TPU v7x, 256 devices: a whole 4x4x8 slice. The times are simulated.
256 devices in a mesh: gx: 8 (over y, core), gy: 4 (over z_lo), gz: 8 (over x, z_hi).
Axes of the slice: x: 4, y: 4, z: 8 (z_hi: 2, z_lo: 4; z = z_hi * 4 + z_lo), core: 2. Of those that a mesh axis runs over, the one named last changes fastest.
Arguments:
- stream: bfloat16 [65536, 8192], P(('gx', 'gy', 'gz')), may hold values from -4 to 4
- segment_ids: int32 [65536], P(('gx', 'gy', 'gz')), may hold values from 0 to 65535, as said below
- positions: int32 [65536], P(('gx', 'gy', 'gz')), may hold values from 0 to 255, as said below
- norm_gain: bfloat16 [1, 8192], P(None, ('gx', 'gy', 'gz')), may hold values from 0.099609375 to 1.8984375
- q_weight: bfloat16 [1, 8192, 512], P(None, ('gx', 'gy', 'gz')), as said below
- k_weight: bfloat16 [1, 8192, 128], P(None, ('gx', 'gy', 'gz')), as said below
- v_weight: bfloat16 [1, 8192, 128], P(None, ('gx', 'gy', 'gz')), may hold values from -0.0625 to 0.0625
- o_weight: bfloat16 [1, 512, 8192], P(None, None, ('gx', 'gy', 'gz')), may hold values from -0.25 to 0.25
Outputs:
- result: bfloat16 [65536, 8192], P(('gx', 'gy', 'gz'))
Inputs may be any that keep to these rules, and one draw needn't show every extreme that they name: `segment_ids`: each token's id is the index of its document's first token, so ids never fall along the tokens; every document lies inside one aligned block of 256 tokens, every block starts a new document, and the last token is a document of its own. `positions`: counts from 0 at a document's first token and rises by one per token. `q_weight`: A projection scaled by its fan-in. `k_weight`: A projection scaled by its fan-in.
All inputs are finite; a program needn't handle non-finite values.
Results may differ from a plain program's by a relative error of at most 0.0064.
Values may be sent and summed in bfloat16 or wider, within the bound.
No kernel may reach another device: no remote copies, remote signals or barrier semaphores. Data moves between devices by JAX's collectives and lax.ppermute only.
A program may use at most 128 MiB of HBM per device.

v0:
```python
import math

import jax
import jax.numpy as jnp
from jax import lax
from jax.sharding import PartitionSpec as P


def in_one_piece(arrays, axis, dim, along):
    widths = [math.prod(a.shape[along:]) for a in arrays]
    both = jnp.concatenate(
        [a.reshape(*a.shape[:along], w) for a, w in zip(arrays, widths)], axis=along
    )
    whole = lax.all_gather(both, axis, axis=dim, tiled=True)
    parts = jnp.split(whole, [sum(widths[:k]) for k in range(1, len(widths))], axis=along)
    return tuple((b.reshape(*whole.shape[:along], *a.shape[along:]) for a, b in zip(arrays, parts)))


def joined_along(parts, dim):
    parts = jnp.moveaxis(parts, 0, dim)
    dims = parts.shape
    return parts.reshape(*dims[:dim], dims[dim] * dims[dim + 1], *dims[dim + 2 :])


def sent_to_all(shard, axis):
    length = lax.axis_size(axis)
    return lax.all_to_all(
        jnp.broadcast_to(shard[None], (length, *shard.shape)), axis, 0, 0, tiled=True
    )


def collect(shard, axis, dim):
    return joined_along(sent_to_all(shard, axis), dim)


def in_one_piece_2(arrays, axis, dim, along):
    columns = [a.reshape(*a.shape[:along], -1) for a in arrays]
    both = jnp.concatenate(columns, axis=along)
    whole, at, gathered = (collect(both, axis, dim), 0, [])
    for a, column in zip(arrays, columns):
        slab = whole[..., at : at + column.shape[along]]
        gathered.append(slab.reshape(*slab.shape[:along], *a.shape[along:]))
        at += column.shape[along]
    return tuple(gathered)


def rotate(values, positions):
    width = values.shape[-1]
    half = width // 2
    freqs = jnp.exp(-math.log(500000.0) * jnp.arange(half, dtype=jnp.float32) * 2.0 / width)
    angles = positions.astype(jnp.float32)[:, None] * freqs[None, :]
    cosine = jnp.concatenate([jnp.cos(angles), jnp.cos(angles)], -1)[:, None, :]
    sine = jnp.concatenate([jnp.sin(angles), jnp.sin(angles)], -1)[:, None, :]
    turned = jnp.concatenate([-values[..., half:], values[..., :half]], -1)
    return values * cosine + turned * sine


def attend(queries, keys, values, segment_ids, positions):
    count = queries.shape[0]
    scores = jnp.einsum(
        "thd,sd->hts", queries, keys, preferred_element_type=jnp.float32
    ) / math.sqrt(keys.shape[-1])
    allowed = (segment_ids[:, None] == segment_ids[None, :]) & (
        positions[None, :] <= positions[:, None]
    )
    scores = jnp.where(allowed[None], scores, -1e30)
    peak = jnp.max(scores, -1, keepdims=True)
    expd = jnp.exp(scores - peak)
    probs = (expd / jnp.sum(expd, -1, keepdims=True)).astype(jnp.bfloat16)
    mixed = jnp.einsum("hts,sd->thd", probs, values, preferred_element_type=jnp.float32)
    return mixed.astype(jnp.bfloat16).reshape(count, -1)


def body(stream, segment_ids, positions, norm_gain, q_weight, k_weight, v_weight, o_weight):
    count = stream.shape[0]
    head_size = k_weight.shape[2]
    current = stream
    widened = lax.optimization_barrier(current).astype(jnp.float32)
    inverse = lax.rsqrt(jnp.mean(widened * widened, -1, keepdims=True) + 1e-05)
    scaled = widened * inverse
    inner = in_one_piece((norm_gain[0], q_weight[0], k_weight[0], v_weight[0]), "gz", 0, 1)
    middle = in_one_piece_2((inner[0], inner[1], inner[2], inner[3]), "gy", 0, 1)
    gain_piece, query_piece, key_piece, value_piece = in_one_piece(
        (middle[0], middle[1], middle[2], middle[3]), "gx", 0, 1
    )
    normed = (scaled * gain_piece.astype(jnp.float32)[None, :]).astype(jnp.bfloat16)
    query_raw = jnp.dot(normed, query_piece, preferred_element_type=jnp.float32)
    key_raw = jnp.dot(normed, key_piece, preferred_element_type=jnp.float32)
    value_raw = jnp.dot(normed, value_piece, preferred_element_type=jnp.float32)
    queries = rotate(query_raw.reshape(count, -1, head_size), positions).astype(jnp.bfloat16)
    keys = rotate(key_raw[:, None, :], positions)[:, 0, :].astype(jnp.bfloat16)
    values = value_raw.astype(jnp.bfloat16)
    mixed = attend(queries, keys, values, segment_ids, positions)
    inner_cols = collect(o_weight[0], "gz", 1)
    middle_cols = collect(inner_cols, "gy", 1)
    branch = jnp.dot(
        mixed,
        lax.all_gather(middle_cols, "gx", axis=1, tiled=True),
        preferred_element_type=jnp.float32,
    )
    current = (widened + branch).astype(jnp.bfloat16)
    return current


def solution(mesh):
    in_specs = (
        P(("gx", "gy", "gz"), None),
        P(("gx", "gy", "gz")),
        P(("gx", "gy", "gz")),
        P(None, ("gx", "gy", "gz")),
        P(None, ("gx", "gy", "gz"), None),
        P(None, ("gx", "gy", "gz"), None),
        P(None, ("gx", "gy", "gz"), None),
        P(None, None, ("gx", "gy", "gz")),
    )
    out_specs = P(("gx", "gy", "gz"), None)
    return jax.shard_map(body, mesh=mesh, in_specs=in_specs, out_specs=out_specs, check_vma=False)
```

profile of v0, /device:TPU:1, one launch (start us, length us, event | category | flops | bytes accessed | tf_op | source)
XLA Modules:
  0.0 239.6 jit_solution(15348834495448399138)
XLA Ops:
  6.5 0.7 copy.31
  7.3 0.9 pad_maximum_fusion.2
  8.2 43.9 %all_gather.9 = bf16[256,769]{1,0:T(8,128)(2,1)S(1)} all-gather(bf16[32,769]{1,0:T(8,128)(2,1)S(1)} %pad_maximum_fusion.2), channel_id=1, replica_groups=mesh['gx'=8,'gy'=4,'gz'=8] {'gz'}, dimensions={0}, use_global_device_ids=true | all-gather | bytes 442944 | tf_op jit(solution)/shard_map/all_gather | solution.py:14
  52.1 0.2 copy.32
  52.4 39.5 %all_to_all.15 = bf16[4,256,769]{1,2,0:T(8,128)(2,1)S(1)} all-to-all(bf16[4,256,769]{1,2,0:T(8,128)(2,1)S(1)} %broadcast_in_dim.20), channel_id=1, replica_groups=mesh['gx'=8,'gy'=4,'gz'=8] {'gy'}, dimensions={0} | all-to-all | bytes 3149824 | tf_op jit(solution)/shard_map/all_to_all | solution.py:27
  92.0 0.6 copy.72
  92.6 0.6 pad.12
  93.2 1.5 copy.46
  94.8 19.0 %all_to_all.16 = bf16[8,512,32]{1,2,0:T(8,128)(2,1)S(1)} all-to-all(bf16[8,512,32]{1,2,0:T(8,128)(2,1)S(1)} %broadcast_in_dim.29), channel_id=1, replica_groups=mesh['gx'=8,'gy'=4,'gz'=8] {'gz'}, dimensions={0} | all-to-all | bytes 524288 | tf_op jit(solution)/shard_map/all_to_all | solution.py:27
  113.9 27.3 %all_to_all.17 = bf16[4,512,256]{1,2,0:T(8,128)(2,1)} all-to-all(bf16[4,512,256]{1,2,0:T(8,128)(2,1)S(1)} %broadcast_in_dim.31), channel_id=1, replica_groups=mesh['gx'=8,'gy'=4,'gz'=8] {'gy'}, dimensions={0} | all-to-all | bytes 2097152 | tf_op jit(solution)/shard_map/all_to_all | solution.py:27
  141.3 3.3 %fusion.2 = f32[256]{0:T(256)S(1)} fusion(bf16[256,8192]{1,0:T(8,128)(2,1)} %param.8), kind=kLoop, calls=%fused_computation.5 | loop fusion | flops 6291200 | bytes 4195328 | tf_op jit(solution)/shard_map/reduce_sum | solution.py:79
  144.6 0.1 compare_and_fusion
  144.7 0.3 multiply_cosine_fusion
  145.1 24.2 %all-gather.3.cloned.1.call-done = bf16[8192,769]{0,1:T(8,128)(2,1)} async-done(((bf16[1024,769]{0,1:T(8,128)(2,1)}), bf16[8192,769]{0,1:T(8,128)(2,1)}) %all-gather.3.cloned.1.call-update) | async-done | bytes 12599312 | tf_op jit(solution)/shard_map/all_gather | solution.py:14
  169.2 0.9 slice_convert_fusion
  170.2 4.7 %fusion.7 = f32[256,128]{0,1:T(8,128)S(1)} fusion(bf16[8192,769]{0,1:T(8,128)(2,1)} %all-gather.3.cloned.1.call-done, bf16[256,8192]{1,0:T(8,128)(2,1)} %param.8, f32[8192]{0:T(1024)S(1)} %bitcast.91, f32[256]{0:T(256)S(1)} %add_rsqrt_fusion), kind=kOutput, calls=%fused_computation.10 | convolution fusion | flops 545259520 | bytes 6456320 | tf_op jit(solution)/shard_map/dot_general | solution.py:88
  175.0 7.8 %fusion.5 = f32[256,512]{1,0:T(8,128)S(1)} fusion(bf16[8192,769]{0,1:T(8,128)(2,1)} %all-gather.3.cloned.1.call-done, bf16[256,8192]{1,0:T(8,128)(2,1)} %param.8, f32[8192]{0:T(1024)S(1)} %bitcast.92, f32[256]{0:T(256)S(1)} %add_rsqrt_fusion), kind=kOutput, calls=%fused_computation.8 | convolution fusion | flops 2155872256 | bytes 13140992 | tf_op jit(solution)/shard_map/dot_general | solution.py:87
  182.8 0.2 reshape.109
  183.0 0.3 slice_negate_fusion
  183.4 0.4 maximum_multiply_fusion
  183.8 0.5 fusion.43
  184.4 5.5 %convolution_convert_fusion = bf16[128,4,256]{2,0,1:T(8,128)(2,1)S(1)} fusion(bf16[8192,769]{0,1:T(8,128)(2,1)} %all-gather.3.cloned.1.call-done, f32[4,256,256]{1,2,0:T(8,128)S(1)} %get-tuple-element.15, f32[4,256]{1,0:T(4,128)S(1)} %get-tuple-element.14, bf16[256,8192]{1,0:T(8,128)(2,1)} %param.8, f32[8192]{0:T(1024)S(1)} %bitcast.93, ...), kind=kOutput, calls=%fused_computation.20 | convolution fusion | flops 613056512 | bytes 7640064 | tf_op jit(solution)/shard_map/hts,sd->thd/dot_general | solution.py:70
  189.9 33.8 %all-gather.5.cloned.1.call-done = bf16[512,8192]{0,1:T(8,128)(2,1)} async-done(((bf16[512,1024]{0,1:T(8,128)(2,1)}), bf16[512,8192]{0,1:T(8,128)(2,1)}) %all-gather.5.cloned.1.call-update) | async-done | bytes 8388624 | tf_op jit(solution)/shard_map/all_gather | solution.py:98
  223.7 9.0 %fusion.1 = bf16[256,8192]{1,0:T(8,128)(2,1)} fusion(bf16[256,512]{0,1:T(8,128)(2,1)S(1)} %bitcast.88, bf16[512,8192]{0,1:T(8,128)(2,1)} %all-gather.5.cloned.1.call-done, bf16[256,8192]{1,0:T(8,128)(2,1)} %param.8), kind=kOutput, calls=%fused_computation.4 | convolution fusion | flops 2153775104 | bytes 17039360 | tf_op jit(solution)/shard_map/dot_general | solution.py:96
  (21 shorter events, 0.6 us)
Async XLA Ops:
  6.5 162.7 %all-gather.3.cloned.1.call-start = ((), (), s32[]{:S(2)}) async-start(), calls=%async_computation.3 | async-start | bytes 14303232 | tf_op jit(solution)/shard_map/all_gather | solution.py:14
  52.1 42.7 %copy-start = (bf16[1,512,32]{1,2,0:T(8,128)(2,1)S(1)}, bf16[1,512,32]{1,2,0:T(8,128)(2,1)}, u32[]{:S(2)}) copy-start(bf16[1,512,32]{1,2,0:T(8,128)(2,1)} %param.15) | copy-start | bytes 98308
  92.0 49.3 %copy-start.1 = (s32[256]{0:T(256)S(1)}, s32[256]{0:T(256)}, u32[]{:S(2)}) copy-start(s32[256]{0:T(256)} %param.10) | copy-start | bytes 3076
  92.6 52.0 %copy-start.2 = (s32[256]{0:T(256)S(1)}, s32[256]{0:T(256)}, u32[]{:S(2)}) copy-start(s32[256]{0:T(256)} %param.9) | copy-start | bytes 3076
  94.7 129.0 %all-gather.5.cloned.1.call-start = ((), (), s32[]{:S(2)}) async-start(), calls=%async_computation.4 | async-start | bytes 9437184 | tf_op jit(solution)/shard_map/all_gather | solution.py:98
Sparse Core Ops, SparseCore 0:
  94.9 74.3 all-gather.2
  171.1 52.6 all-gather.4
where the time goes:
time: 240 us
  blocking collectives  130 us (54%)
  waiting for transfers between devices  58 us (24%)
  matrix products  27.5 us (11%)
  between operations  13.6 us (6%)
  other arithmetic  6.33 us (3%)
  local copies, waits for them, and re-layouts  4.32 us (2%)
    all_to_all x3, blocking collectives, sent_to_all(): lax.all_to_all(jnp.broadcast_to(shard[None], (length, *shard.shape)), axi...  85.8 us
    all_gather x1, blocking collectives, in_one_piece(): whole = lax.all_gather(both, axis, axis=dim, tiled=True)  43.9 us
    all_gather x1, waiting for transfers between devices, body(): lax.all_gather(middle_cols, 'gx', axis=1, tiled=True)  33.8 us
    all_gather x1, waiting for transfers between devices, in_one_piece(): whole = lax.all_gather(both, axis, axis=dim, tiled=True)  24.2 us
    dot_general x1, matrix products, body(): jnp.dot(mixed, lax.all_gather(middle_cols, 'gx', axis=1, tiled=True), pre...  9 us
    dot_general x1, matrix products, body(): query_raw = jnp.dot(normed, query_piece, preferred_element_type=jnp.float32)  7.75 us
    dot_general x1, matrix products, attend(): jnp.einsum('hts,sd->thd', probs, values, preferred_element_type=jnp.float32)  5.54 us
  transfers between devices with their start and end apart: 2, of which 2 were waited for; matrix products, arithmetic and copies ran while one was open for 10% of the time, Pallas kernels for 0%

commit v1 on v0

v1 whole, which is shorter than its diff:
```python
import functools
import math

import jax
import jax.numpy as jnp
from jax import lax
from jax.experimental import pallas as pl
from jax.experimental.pallas import tpu as pltpu
from jax.sharding import Mesh, PartitionSpec as P

AXES = ("y", "c", "zl", "x", "zh")
NY, NC, NZL, NX, NZH = 4, 2, 4, 4, 2
HD = 128
ROWS = 32
T = 256


def rope(h, cos, sin):
    return h * cos + pltpu.roll(h, HD // 2, 1) * sin


def attend_kernel(x_ref, w0_ref, w1_ref, w2_ref, inv_ref, cos_ref, sin_ref, mask_ref, out_ref, acc_ref):
    step = pl.program_id(0)

    @pl.when(step == 0)
    def _():
        acc_ref[...] = jnp.zeros_like(acc_ref)

    for n, w_ref in enumerate((w0_ref, w1_ref, w2_ref)):
        total = acc_ref[:, n * 256 : n * 256 + 256]
        for zl in range(NZL):
            rows = w_ref[0, :, 0, :, zl].reshape(NX * NZH * ROWS, 256)
            total += jnp.dot(x_ref[:, zl * 256 : zl * 256 + 256], rows, preferred_element_type=jnp.float32)
        acc_ref[:, n * 256 : n * 256 + 256] = total

    @pl.when(step == pl.num_programs(0) - 1)
    def _():
        inv, cos, sin = inv_ref[...], cos_ref[...], sin_ref[...]
        allowed = mask_ref[...] > 0
        keys = rope(acc_ref[:, 512:640] * inv, cos, sin).astype(jnp.bfloat16)
        values = (acc_ref[:, 640:768] * inv).astype(jnp.bfloat16)
        for h in range(4):
            q = rope(acc_ref[:, h * HD : h * HD + HD] * inv, cos, sin).astype(jnp.bfloat16)
            s = lax.dot_general(q, keys, (((1,), (1,)), ((), ())), preferred_element_type=jnp.float32)
            s = jnp.where(allowed, s * (1.0 / math.sqrt(HD)), -1e30)
            e = jnp.exp(s - jnp.max(s, -1, keepdims=True))
            probs = (e / jnp.sum(e, -1, keepdims=True)).astype(jnp.bfloat16)
            out_ref[:, h * HD : h * HD + HD] = jnp.dot(
                probs, values, preferred_element_type=jnp.float32
            ).astype(jnp.bfloat16)


def project_kernel(mixed_ref, x_ref, w3_ref, w4_ref, out_ref):
    for zl in range(NZL):
        total = x_ref[:, zl * 256 : zl * 256 + 256].astype(jnp.float32)
        for n, w_ref in enumerate((w3_ref, w4_ref)):
            rows = w_ref[0, :, 0, :, zl].reshape(NX * NZH * ROWS, 256)
            total += lax.dot_general(
                mixed_ref[:, n * 256 : n * 256 + 256],
                rows,
                (((1,), (1,)), ((), ())),
                preferred_element_type=jnp.float32,
            )
        out_ref[:, zl * 256 : zl * 256 + 256] = total.astype(jnp.bfloat16)


def weight_spec(col):
    return pl.BlockSpec(
        (1, NX, 1, NZH, NZL, ROWS, 256), lambda s: (s // NC, 0, s % NC, 0, 0, 0, col)
    )


def body(stream, segment_ids, positions, norm_gain, q_weight, k_weight, v_weight, o_weight):
    gain = norm_gain[0].astype(jnp.float32)[:, None]
    qkv = jnp.concatenate([q_weight[0], k_weight[0], v_weight[0]], -1)
    qkv = (qkv.astype(jnp.float32) * gain).astype(jnp.bfloat16)
    local = jnp.concatenate([qkv, o_weight[0].T], -1)
    column = lax.all_gather(local, ("zh", "zl"), axis=0, tiled=True)
    whole = lax.all_gather(column, ("y", "x", "c"), axis=0, tiled=True)
    whole = whole.reshape(NY, NX, NC, NZH, NZL, ROWS, 1280)

    wide = stream.astype(jnp.float32)
    inv = lax.rsqrt(jnp.mean(wide * wide, -1, keepdims=True) + 1e-05)
    freqs = jnp.exp(-math.log(500000.0) * jnp.arange(HD // 2, dtype=jnp.float32) * 2.0 / HD)
    angles = positions.astype(jnp.float32)[:, None] * freqs[None, :]
    cos, sin = jnp.cos(angles), jnp.sin(angles)
    cos = jnp.concatenate([cos, cos], -1)
    sin = jnp.concatenate([-sin, sin], -1)
    allowed = (segment_ids[:, None] == segment_ids[None, :]) & (positions[None, :] <= positions[:, None])
    mask = allowed.astype(jnp.float32)

    steps = NY * NC
    whole_block = lambda shape: pl.BlockSpec(shape, lambda s: (0, 0))
    mixed = pl.pallas_call(
        attend_kernel,
        grid=(steps,),
        in_specs=[
            pl.BlockSpec((T, 1024), lambda s: (0, s)),
            weight_spec(0),
            weight_spec(1),
            weight_spec(2),
            whole_block((T, 1)),
            whole_block((T, HD)),
            whole_block((T, HD)),
            whole_block((T, T)),
        ],
        out_specs=whole_block((T, 512)),
        out_shape=jax.ShapeDtypeStruct((T, 512), jnp.bfloat16),
        scratch_shapes=[pltpu.VMEM((T, 768), jnp.float32)],
        compiler_params=pltpu.CompilerParams(dimension_semantics=("arbitrary",)),
        name="attend",
    )(stream, whole, whole, whole, inv, cos, sin, mask)
    return pl.pallas_call(
        project_kernel,
        grid=(steps,),
        in_specs=[
            whole_block((T, 512)),
            pl.BlockSpec((T, 1024), lambda s: (0, s)),
            weight_spec(3),
            weight_spec(4),
        ],
        out_specs=pl.BlockSpec((T, 1024), lambda s: (0, s)),
        out_shape=jax.ShapeDtypeStruct((T, 8192), jnp.bfloat16),
        compiler_params=pltpu.CompilerParams(dimension_semantics=("arbitrary",)),
        name="project",
    )(mixed, stream, whole, whole)


def solution(mesh):
    fine = Mesh(mesh.devices.reshape(NY, NC, NZL, NX, NZH), AXES)
    in_specs = (
        P(AXES, None),
        P(AXES),
        P(AXES),
        P(None, AXES),
        P(None, AXES, None),
        P(None, AXES, None),
        P(None, AXES, None),
        P(None, None, AXES),
    )
    return jax.shard_map(body, mesh=fine, in_specs=in_specs, out_specs=P(AXES, None), check_vma=False)
```

time: 240 us -> 158 us (0.66)
  blocking collectives: 130 us -> 26.6 us
  matrix products: 27.5 us -> 0 us
  waiting for transfers between devices: 58 us -> 85.3 us
  Pallas kernels: 0 us -> 22.1 us
  local copies, waits for them, and re-layouts: 4.32 us -> 0.81 us
  other arithmetic: 6.33 us -> 9.09 us
    all_to_all x3 -> x0, blocking collectives: 85.8 us -> none  [sent_to_all(): lax.all_to_all(jnp.broadcast_to(shard[None], (length, *shard.shape)), axi...]
    all_gather x2 -> x1, waiting for transfers between devices: 58 us -> 85.2 us  [body(): whole = lax.all_gather(column, ('y', 'x', 'c'), axis=0, tiled=True)]
    dot_general x4 -> x0, matrix products: 27 us -> none  [the longest x1 9 us: body(): jnp.dot(mixed, lax.all_gather(middle_cols, 'gx', axis=1, tiled=True), pre...]
    pallas_call x0 -> x2, Pallas kernels: none -> 22.1 us  [the longest x1 12 us: body(): pl.pallas_call(attend_kernel, grid=(steps,), in_specs=[pl.BlockSpec((T, 1...]
    all_gather x1, blocking collectives: 43.9 us -> 26.6 us  [body(): column = lax.all_gather(local, ('zh', 'zl'), axis=0, tiled=True)]
    convert_element_type x2 -> x4, other arithmetic: 0.93 us -> 3.82 us  [the longest x1 1.61 us: body(): mask = allowed.astype(jnp.float32)]
  transfers between devices with their start and end apart: 2 -> 1, of which waited for: 2 -> 1; matrix products, arithmetic and copies ran while one was open for 10% -> 5% of each run, Pallas kernels for 0% -> 0%
where the time goes in v1:
time: 158 us; the launch traced here: 157 us
  waiting for transfers between devices  85.3 us (54%)
  blocking collectives  26.6 us (17%)
  Pallas kernels  22.1 us (14%)
  between operations  13.4 us (8%)
  other arithmetic  9.09 us (6%)
    all_gather x1, waiting for transfers between devices, body(): whole = lax.all_gather(column, ('y', 'x', 'c'), axis=0, tiled=True)  85.2 us
    all_gather x1, blocking collectives, body(): column = lax.all_gather(local, ('zh', 'zl'), axis=0, tiled=True)  26.6 us
    pallas_call x1, Pallas kernels, body(): pl.pallas_call(attend_kernel, grid=(steps,), in_specs=[pl.BlockSpec((T, 1...  12 us
    pallas_call x1, Pallas kernels, body(): pl.pallas_call(project_kernel, grid=(steps,), in_specs=[whole_block((T, 5...  10.1 us
  transfers between devices with their start and end apart: 1, of which 1 were waited for; matrix products, arithmetic and copies ran while one was open for 5% of the time, Pallas kernels for 0%

profile of v1, /device:TPU:1, one launch (start us, length us, event | category | flops | bytes accessed | tf_op | source)
XLA Modules:
  0.0 157.2 jit_solution(4187165293277077436)
XLA Ops:
  6.5 0.0 all-gather.2.cloned.1.call-start
  6.5 0.7 bitcast_convert_fusion
  7.2 0.9 multiply_convert_fusion
  8.1 0.8 pad_maximum_fusion.2
  8.8 26.6 %all_gather.6 = bf16[256,1280]{1,0:T(8,128)(2,1)} all-gather(bf16[32,1280]{1,0:T(8,128)(2,1)S(1)} %pad_maximum_fusion.2), channel_id=1, replica_groups=mesh['y'=4,'c'=2,'zl'=4,'x'=4,'zh'=2] {'zh','zl'}, dimensions={0}, use_global_device_ids=true | all-gather | bytes 737280 | tf_op jit(solution)/shard_map/all_gather | solution.py:78
  35.4 0.0 all-gather.2.cloned.1.call-update
  35.4 0.7 convert_element_type.30
  36.1 3.1 %multiply_reduce_fusion = f32[256]{0:T(256)S(1)} fusion(bf16[256,8192]{1,0:T(8,128)(2,1)} %x_ref.3), kind=kLoop, calls=%fused_computation | loop fusion | flops 6291200 | bytes 4195328 | tf_op jit(solution)/shard_map/reduce_sum | solution.py:83
  39.2 0.8 copy.9.inv_ref
  40.1 0.5 fusion
  40.6 0.8 pad_maximum_fusion
  41.5 1.6 %and_convert_fusion.mask_ref = f32[256,256]{1,0:T(8,128)} fusion(s32[256]{0:T(256)} %param.10, s32[256]{0:T(256)} %param.9), kind=kLoop, calls=%fused_computation.1 | loop fusion | flops 262144 | bytes 264192 | tf_op jit(solution)/shard_map/convert_element_type | solution.py:90
  43.1 85.2 %all-gather.2.cloned.1.call-done = bf16[8192,1280]{1,0:T(8,128)(2,1)} async-done(((bf16[256,1280]{1,0:T(8,128)(2,1)}), bf16[8192,1280]{1,0:T(8,128)(2,1)}) %all-gather.2.cloned.1.call-update) | async-done | bytes 20971536 | tf_op jit(solution)/shard_map/all_gather | solution.py:79
  128.3 12.0 %attend.1.mixed_ref = bf16[256,512]{1,0:T(8,128)(2,1)} custom-call(bf16[256,8192]{1,0:T(8,128)(2,1)} %x_ref.3, bf16[4,4,2,2,4,32,1280]{6,5,4,3,2,1,0:T(8,128)(2,1)} %bitcast.11, bf16[4,4,2,2,4,32,1280]{6,5,4,3,2,1,0:T(8,128)(2,1)} %bitcast.12, bf16[4,4,2,2,4,32,1280]{6,5,4,3,2,1,0:T(8,128)(2,1)} %bitcast.13, f32[256,1]{1,0:T(8,128)} %copy.9.inv_ref, ...), custom_call_target="tpu_custom_call" | custom-call | tf_op jit(solution)/shard_map/attend/pallas_call | solution.py:94
  140.3 10.1 %project.1 = bf16[256,8192]{1,0:T(8,128)(2,1)} custom-call(bf16[256,512]{1,0:T(8,128)(2,1)} %attend.1.mixed_ref, bf16[256,8192]{1,0:T(8,128)(2,1)} %x_ref.3, bf16[4,4,2,2,4,32,1280]{6,5,4,3,2,1,0:T(8,128)(2,1)} %bitcast.14, bf16[4,4,2,2,4,32,1280]{6,5,4,3,2,1,0:T(8,128)(2,1)} %bitcast.15), custom_call_target="tpu_custom_call" | custom-call | tf_op jit(solution)/shard_map/project/pallas_call | solution.py:113
  (2 shorter events, 0.0 us)
Async XLA Ops:
  6.5 121.8 %all-gather.2.cloned.1.call-start = ((), (), s32[]{:S(2)}) async-start(), calls=%async_computation | async-start | bytes 21626880 | tf_op jit(solution)/shard_map/all_gather | solution.py:79
Sparse Core Ops, SparseCore 0:
  35.6 92.6 all-gather.1
